TPU v7x, 32 devices: a whole 2x2x4 slice. The times are simulated.
32 devices in a mesh: blk: 8 (over z, x), grp: 4 (over y, core).
Axes of the slice: x: 2, y: 2, z: 4, core: 2. Of those that a mesh axis runs over, the one named last changes fastest.
Arguments:
- sources: bfloat16 [8192, 256], P('blk'), may hold values from -64 to 64
- positive: int32 [8192], P('blk'), may hold values from 0 to 8191
- src_part: int32 [8192], P('blk'), may hold values from 0 to 7
- destinations: bfloat16 [8192, 256], P(('blk', 'grp')), may hold values from -8 to 8
- dst_part: int32 [8192], P(('blk', 'grp')), may hold values from 0 to 7
Outputs:
- loss: float32 [8192], P('blk')
All inputs are finite; a program needn't handle non-finite values.
Results may differ from a plain program's by a relative error of at most 0.0003.
Values may be sent and summed in bfloat16 or wider, within the bound.
No kernel may reach another device: no remote copies, remote signals or barrier semaphores. Data moves between devices by JAX's collectives and lax.ppermute only.
A program may use at most 192 MiB of HBM per device.

v0:
```python
import jax
import jax.numpy as jnp
from jax import lax
from jax.sharding import PartitionSpec as P

SCALE = 3.0
NEG = -1e30


def passed_along(block, axis, distance):
    devices = range(lax.axis_size(axis))
    route = [((i - distance) % len(devices), i) for i in devices]
    return lax.ppermute(block, axis, route)


def merged(value, axis, join):
    pieces = jax.tree.map(lambda part: lax.all_gather(part, axis), value)
    head = jax.tree.map(lambda part: part[0], pieces)
    tail = jax.tree.map(lambda part: part[1:], pieces)
    so_far, _ = lax.scan(lambda so_far, section: (join(so_far, section), None), head, tail)
    return so_far


def global_columns(row_start, count, width, group, groups):
    flat = row_start + jnp.arange(count, dtype=jnp.int32)
    return flat // width * (groups * width) + group * width + flat % width


def score_block(carry, sources, positive, src_part, block, block_part, columns):
    maxima, totals, pos_logit = carry
    logits = SCALE * lax.dot_general(
        sources, block, (((1,), (1,)), ((), ())), preferred_element_type=jnp.float32
    )
    is_pos = columns[None, :] == positive[:, None]
    keep = (block_part[None, :] != src_part[:, None]) | is_pos
    masked = jnp.where(keep, logits, NEG)
    new_max = jnp.maximum(maxima, jnp.max(masked, axis=1))
    weights = jnp.where(keep, jnp.exp(masked - new_max[:, None]), 0.0)
    totals = totals * jnp.exp(maxima - new_max) + jnp.sum(weights, axis=1)
    pos_logit = pos_logit + jnp.sum(jnp.where(is_pos, logits, 0.0), axis=1)
    return (new_max, totals, pos_logit)


def combine(first, second):
    max_a, sum_a, pos_a = first
    max_b, sum_b, pos_b = second
    top = jnp.maximum(max_a, max_b)
    return (top, sum_a * jnp.exp(max_a - top) + sum_b * jnp.exp(max_b - top), pos_a + pos_b)


def on_device(sources, positive, src_part, destinations, dst_part):
    width = destinations.shape[0]
    count_rows = sources.shape[0]
    groups = lax.axis_size("grp")
    group = lax.axis_index("grp")
    cycle = lax.axis_size("blk")
    here = lax.axis_index("blk")
    start = (
        jnp.full((count_rows,), NEG, jnp.float32),
        jnp.zeros((count_rows,), jnp.float32),
        jnp.zeros((count_rows,), jnp.float32),
    )

    def fold_rows(carry, block, block_part, row_start):
        columns = global_columns(row_start, block.shape[0], width, group, groups)
        return score_block(carry, sources, positive, src_part, block, block_part, columns)

    half = cycle // 2
    carry = fold_rows(start, destinations, dst_part, here * width)

    def turn_both(step, state):
        carry, fwd_block, fwd_part, back_block, back_part = state
        fwd_block, fwd_part = passed_along((fwd_block, fwd_part), "blk", 1)
        back_block, back_part = passed_along((back_block, back_part), "blk", -1)
        carry = fold_rows(carry, fwd_block, fwd_part, (here - step) % cycle * width)
        carry = lax.cond(
            step < half,
            lambda value: fold_rows(value, back_block, back_part, (here + step) % cycle * width),
            lambda value: value,
            carry,
        )
        return (carry, fwd_block, fwd_part, back_block, back_part)

    state = lax.fori_loop(
        1, half + 1, turn_both, (carry, destinations, dst_part, destinations, dst_part)
    )
    carry = state[0]
    maxima, totals, pos_logit = merged(carry, "grp", combine)
    return maxima + jnp.log(totals) - pos_logit


def solution(mesh):
    return jax.shard_map(
        on_device,
        mesh=mesh,
        in_specs=(P("blk", None), P("blk"), P("blk"), P(("blk", "grp"), None), P(("blk", "grp"))),
        out_specs=P("blk"),
        check_vma=False,
    )
```

profile of v0, /device:TPU:0, one launch (start us, length us, event | category | flops | bytes accessed | tf_op | source)
XLA Modules:
  0.0 67.6 jit_solution(9549519580292324987)
XLA Ops:
  2.3 1.4 %fusion.10 = (f32[1024]{0:T(1024)S(1)}, f32[1024,256]{0,1:T(8,128)S(1)}) fusion(s32[1024]{0:T(1024)S(1)} %copy-done, s32[1024]{0:T(1024)S(1)} %copy-done.1, s32[256]{0:T(256)S(1)} %fusion.11, s32[256]{0:T(256)S(1)} %copy.52, bf16[1024,256]{1,0:T(8,128)(2,1)} %param.11, bf16[256,256]{1,0:T(8,128)(2,1)S(1)} %copy.51), kind=kOutput, calls=%fused_computation.38 | convolution fusion | flops 135789568 | bytes 1718272 | tf_op jit(solution)/shard_map/dot_general | solution.py:31
  4.8 45.6 %while.42 = (s32[]{:T(128)}, f32[1024]{0:T(1024)S(1)}, f32[1024]{0:T(1024)S(1)}, f32[1024]{0:T(1024)S(1)}, bf16[256,256]{1,0:T(8,128)(2,1)S(1)}, /*index=5*/s32[...) while((s32[]{:T(128)}, f32[1024]{0:T(1024)S(1)}, ...), condition=%wide.region_12.13_spmd, body=%wide.region_3.12_spmd.sunk | while | flops 276315680 | bytes 7273241 | solution.py:84
  4.8 3.0 %collective-permute-start.1 = (bf16[256,256]{1,0:T(8,128)(2,1)S(1)}, bf16[256,256]{1,0:T(8,128)(2,1)S(1)}, u32[]{:S(2)}, u32[]{:S(2)}) collective-permute-start(bf16[256,256]{1,0:T(8,128)(2,1)S(1)} %get-tuple-element.710), channel_id=1, source_target_pairs={{28,0},{0,4},{4,8},{8,12},{12,16},{16,20},{20,24},{24,28},{29,1},{... | collective-permute-start | bytes 393224 | tf_op jit(solution)/shard_map/while/body/eval_jaxpr/ppermute | solution.py:13
  7.7 1.5 %collective-permute-start = (s32[256]{0:T(256)S(1)}, s32[256]{0:T(256)S(1)}, u32[]{:S(2)}, u32[]{:S(2)}) collective-permute-start(s32[256]{0:T(256)S(1)} %get-tuple-element.711), channel_id=1, source_target_pairs={{28,0},{0,4},{4,8},{8,12},{12,16},{16,20},{20,24},{24,28},{29,1},{... | collective-permute-start | bytes 3080 | tf_op jit(solution)/shard_map/while/body/eval_jaxpr/ppermute | solution.py:13
  9.3 3.2 %collective-permute-start.3 = (bf16[256,256]{1,0:T(8,128)(2,1)S(1)}, bf16[256,256]{1,0:T(8,128)(2,1)S(1)}, u32[]{:S(2)}, u32[]{:S(2)}) collective-permute-start(bf16[256,256]{1,0:T(8,128)(2,1)S(1)} %get-tuple-element.712), channel_id=1, source_target_pairs={{4,0},{8,4},{12,8},{16,12},{20,16},{24,20},{28,24},{0,28},{5,1},{9... | collective-permute-start | bytes 393224 | tf_op jit(solution)/shard_map/while/body/eval_jaxpr/ppermute | solution.py:13
  12.8 1.6 %collective-permute-done = s32[256]{0:T(256)S(1)} collective-permute-done((s32[256]{0:T(256)S(1)}, s32[256]{0:T(256)S(1)}, u32[]{:S(2)}, u32[]{:S(2)}) %collective-permute-start) | collective-permute-done | bytes 1056 | tf_op jit(solution)/shard_map/while/body/eval_jaxpr/ppermute | solution.py:13
  14.4 2.4 %collective-permute-done.2 = s32[256]{0:T(256)S(1)} collective-permute-done((s32[256]{0:T(256)S(1)}, s32[256]{0:T(256)S(1)}, u32[]{:S(2)}, u32[]{:S(2)}) %collective-permute-start.2) | collective-permute-done | bytes 1056 | tf_op jit(solution)/shard_map/while/body/eval_jaxpr/ppermute | solution.py:13
  19.0 1.4 %collective-permute-start = (s32[256]{0:T(256)S(1)}, s32[256]{0:T(256)S(1)}, u32[]{:S(2)}, u32[]{:S(2)}) collective-permute-start(s32[256]{0:T(256)S(1)} %get-tuple-element.711), channel_id=1, source_target_pairs={{28,0},{0,4},{4,8},{8,12},{12,16},{16,20},{20,24},{24,28},{29,1},{... | collective-permute-start | bytes 3080 | tf_op jit(solution)/shard_map/while/body/eval_jaxpr/ppermute | solution.py:13
  20.5 3.3 %collective-permute-start.3 = (bf16[256,256]{1,0:T(8,128)(2,1)S(1)}, bf16[256,256]{1,0:T(8,128)(2,1)S(1)}, u32[]{:S(2)}, u32[]{:S(2)}) collective-permute-start(bf16[256,256]{1,0:T(8,128)(2,1)S(1)} %get-tuple-element.712), channel_id=1, source_target_pairs={{4,0},{8,4},{12,8},{16,12},{20,16},{24,20},{28,24},{0,28},{5,1},{9... | collective-permute-start | bytes 393224 | tf_op jit(solution)/shard_map/while/body/eval_jaxpr/ppermute | solution.py:13
  23.8 2.0 %collective-permute-start.2 = (s32[256]{0:T(256)S(1)}, s32[256]{0:T(256)S(1)}, u32[]{:S(2)}, u32[]{:S(2)}) collective-permute-start(s32[256]{0:T(256)S(1)} %get-tuple-element.713), channel_id=1, source_target_pairs={{4,0},{8,4},{12,8},{16,12},{20,16},{24,20},{28,24},{0,28},{5,1},{9... | collective-permute-start | bytes 3080 | tf_op jit(solution)/shard_map/while/body/eval_jaxpr/ppermute | solution.py:13
  25.8 1.2 %collective-permute-done = s32[256]{0:T(256)S(1)} collective-permute-done((s32[256]{0:T(256)S(1)}, s32[256]{0:T(256)S(1)}, u32[]{:S(2)}, u32[]{:S(2)}) %collective-permute-start) | collective-permute-done | bytes 1056 | tf_op jit(solution)/shard_map/while/body/eval_jaxpr/ppermute | solution.py:13
  26.9 1.3 %collective-permute-done.2 = s32[256]{0:T(256)S(1)} collective-permute-done((s32[256]{0:T(256)S(1)}, s32[256]{0:T(256)S(1)}, u32[]{:S(2)}, u32[]{:S(2)}) %collective-permute-start.2) | collective-permute-done | bytes 1056 | tf_op jit(solution)/shard_map/while/body/eval_jaxpr/ppermute | solution.py:13
  29.2 1.0 %conditional.2 = ((f32[1024]{0:T(1024)S(1)}, f32[1024]{0:T(1024)S(1)}, f32[1024]{0:T(1024)S(1)})) conditional(s32[]{:T(128)} %convert_element_type.12, (f32[1024]{0:T(1024)S(1)}, f32[1024]{0:T(1024)S(1)}, f32[1024]{0:T(1024)S(1)}) %tuple.74, (s32[256]{0:T(256)S(1)}, s32[1024]{0:T(1024)S(1)}, s32[]{:T(128)}, s32[]{:T(128)}, s32[]{:T(128)}, ...), branch_computations={%region_7.7_spmd, %region_8.11_spmd} | conditional | flops 138157840 | bytes 2843833 | solution.py:76
  31.4 3.8 %collective-permute-start.3 = (bf16[256,256]{1,0:T(8,128)(2,1)S(1)}, bf16[256,256]{1,0:T(8,128)(2,1)S(1)}, u32[]{:S(2)}, u32[]{:S(2)}) collective-permute-start(bf16[256,256]{1,0:T(8,128)(2,1)S(1)} %get-tuple-element.712), channel_id=1, source_target_pairs={{4,0},{8,4},{12,8},{16,12},{20,16},{24,20},{28,24},{0,28},{5,1},{9... | collective-permute-start | bytes 393224 | tf_op jit(solution)/shard_map/while/body/eval_jaxpr/ppermute | solution.py:13
  35.2 2.0 %collective-permute-start.2 = (s32[256]{0:T(256)S(1)}, s32[256]{0:T(256)S(1)}, u32[]{:S(2)}, u32[]{:S(2)}) collective-permute-start(s32[256]{0:T(256)S(1)} %get-tuple-element.713), channel_id=1, source_target_pairs={{4,0},{8,4},{12,8},{16,12},{20,16},{24,20},{28,24},{0,28},{5,1},{9... | collective-permute-start | bytes 3080 | tf_op jit(solution)/shard_map/while/body/eval_jaxpr/ppermute | solution.py:13
  37.2 1.1 %collective-permute-done = s32[256]{0:T(256)S(1)} collective-permute-done((s32[256]{0:T(256)S(1)}, s32[256]{0:T(256)S(1)}, u32[]{:S(2)}, u32[]{:S(2)}) %collective-permute-start) | collective-permute-done | bytes 1056 | tf_op jit(solution)/shard_map/while/body/eval_jaxpr/ppermute | solution.py:13
  39.8 1.0 %conditional.2 = ((f32[1024]{0:T(1024)S(1)}, f32[1024]{0:T(1024)S(1)}, f32[1024]{0:T(1024)S(1)})) conditional(s32[]{:T(128)} %convert_element_type.12, (f32[1024]{0:T(1024)S(1)}, f32[1024]{0:T(1024)S(1)}, f32[1024]{0:T(1024)S(1)}) %tuple.74, (s32[256]{0:T(256)S(1)}, s32[1024]{0:T(1024)S(1)}, s32[]{:T(128)}, s32[]{:T(128)}, s32[]{:T(128)}, ...), branch_computations={%region_7.7_spmd, %region_8.11_spmd} | conditional | flops 138157840 | bytes 2843833 | solution.py:76
  41.1 1.3 %collective-permute-start = (s32[256]{0:T(256)S(1)}, s32[256]{0:T(256)S(1)}, u32[]{:S(2)}, u32[]{:S(2)}) collective-permute-start(s32[256]{0:T(256)S(1)} %get-tuple-element.711), channel_id=1, source_target_pairs={{28,0},{0,4},{4,8},{8,12},{12,16},{16,20},{20,24},{24,28},{29,1},{... | collective-permute-start | bytes 3080 | tf_op jit(solution)/shard_map/while/body/eval_jaxpr/ppermute | solution.py:13
  42.3 3.5 %collective-permute-start.3 = (bf16[256,256]{1,0:T(8,128)(2,1)S(1)}, bf16[256,256]{1,0:T(8,128)(2,1)S(1)}, u32[]{:S(2)}, u32[]{:S(2)}) collective-permute-start(bf16[256,256]{1,0:T(8,128)(2,1)S(1)} %get-tuple-element.712), channel_id=1, source_target_pairs={{4,0},{8,4},{12,8},{16,12},{20,16},{24,20},{28,24},{0,28},{5,1},{9... | collective-permute-start | bytes 393224 | tf_op jit(solution)/shard_map/while/body/eval_jaxpr/ppermute | solution.py:13
  45.8 1.9 %collective-permute-start.2 = (s32[256]{0:T(256)S(1)}, s32[256]{0:T(256)S(1)}, u32[]{:S(2)}, u32[]{:S(2)}) collective-permute-start(s32[256]{0:T(256)S(1)} %get-tuple-element.713), channel_id=1, source_target_pairs={{4,0},{8,4},{12,8},{16,12},{20,16},{24,20},{28,24},{0,28},{5,1},{9... | collective-permute-start | bytes 3080 | tf_op jit(solution)/shard_map/while/body/eval_jaxpr/ppermute | solution.py:13
  47.7 1.0 %collective-permute-done = s32[256]{0:T(256)S(1)} collective-permute-done((s32[256]{0:T(256)S(1)}, s32[256]{0:T(256)S(1)}, u32[]{:S(2)}, u32[]{:S(2)}) %collective-permute-start) | collective-permute-done | bytes 1056 | tf_op jit(solution)/shard_map/while/body/eval_jaxpr/ppermute | solution.py:13
  50.4 5.2 %all-gather = f32[4096]{0:T(1024)S(1)} all-gather(f32[1024]{0:T(1024)S(1)} %get-tuple-element.466), channel_id=2, replica_groups=mesh['blk'=8,'grp'=4] {'grp'}, dimensions={0}, use_global_device_ids=true | all-gather | bytes 20480 | tf_op jit(solution)/shard_map/all_gather | solution.py:17
  55.6 5.2 %all-gather.1 = f32[4096]{0:T(1024)S(1)} all-gather(f32[1024]{0:T(1024)S(1)} %get-tuple-element.467), channel_id=3, replica_groups=mesh['blk'=8,'grp'=4] {'grp'}, dimensions={0}, use_global_device_ids=true | all-gather | bytes 20480 | tf_op jit(solution)/shard_map/all_gather | solution.py:17
  60.9 5.2 %all-gather.2 = f32[4096]{0:T(1024)S(1)} all-gather(f32[1024]{0:T(1024)S(1)} %get-tuple-element.468), channel_id=4, replica_groups=mesh['blk'=8,'grp'=4] {'grp'}, dimensions={0}, use_global_device_ids=true | all-gather | bytes 20480 | tf_op jit(solution)/shard_map/all_gather | solution.py:17
  (125 shorter events, 15.7 us)
Async XLA Ops:
  1.6 0.7 %copy-start.1 = (s32[1024]{0:T(1024)S(1)}, s32[1024]{0:T(1024)}, u32[]{:S(2)}) copy-start(s32[1024]{0:T(1024)} %param.13) | copy-start | bytes 12292
  1.6 0.7 %copy-start = (s32[1024]{0:T(1024)S(1)}, s32[1024]{0:T(1024)}, u32[]{:S(2)}) copy-start(s32[1024]{0:T(1024)} %param.12) | copy-start | bytes 12292
  3.7 1.0 %copy-start.4 = (bf16[1024,256]{1,0:T(8,128)(2,1)S(1)}, bf16[1024,256]{1,0:T(8,128)(2,1)}, u32[]{:S(2)}) copy-start(bf16[1024,256]{1,0:T(8,128)(2,1)} %param.11) | copy-start | bytes 1572868
  4.8 12.1 %collective-permute-start.1 = (bf16[256,256]{1,0:T(8,128)(2,1)S(1)}, bf16[256,256]{1,0:T(8,128)(2,1)S(1)}, u32[]{:S(2)}, u32[]{:S(2)}) collective-permute-start(bf16[256,256]{1,0:T(8,128)(2,1)S(1)} %get-tuple-element.710), channel_id=1, source_target_pairs={{28,0},{0,4},{4,8},{8,12},{12,16},{16,20},{20,24},{24,28},{29,1},{... | collective-permute-start | bytes 393224 | tf_op jit(solution)/shard_map/while/body/eval_jaxpr/ppermute | solution.py:13
  7.7 6.7 %collective-permute-start = (s32[256]{0:T(256)S(1)}, s32[256]{0:T(256)S(1)}, u32[]{:S(2)}, u32[]{:S(2)}) collective-permute-start(s32[256]{0:T(256)S(1)} %get-tuple-element.711), channel_id=1, source_target_pairs={{28,0},{0,4},{4,8},{8,12},{12,16},{16,20},{20,24},{24,28},{29,1},{... | collective-permute-start | bytes 3080 | tf_op jit(solution)/shard_map/while/body/eval_jaxpr/ppermute | solution.py:13
  9.3 8.6 %collective-permute-start.3 = (bf16[256,256]{1,0:T(8,128)(2,1)S(1)}, bf16[256,256]{1,0:T(8,128)(2,1)S(1)}, u32[]{:S(2)}, u32[]{:S(2)}) collective-permute-start(bf16[256,256]{1,0:T(8,128)(2,1)S(1)} %get-tuple-element.712), channel_id=1, source_target_pairs={{4,0},{8,4},{12,8},{16,12},{20,16},{24,20},{28,24},{0,28},{5,1},{9... | collective-permute-start | bytes 393224 | tf_op jit(solution)/shard_map/while/body/eval_jaxpr/ppermute | solution.py:13
  12.5 4.4 %collective-permute-start.2 = (s32[256]{0:T(256)S(1)}, s32[256]{0:T(256)S(1)}, u32[]{:S(2)}, u32[]{:S(2)}) collective-permute-start(s32[256]{0:T(256)S(1)} %get-tuple-element.713), channel_id=1, source_target_pairs={{4,0},{8,4},{12,8},{16,12},{20,16},{24,20},{28,24},{0,28},{5,1},{9... | collective-permute-start | bytes 3080 | tf_op jit(solution)/shard_map/while/body/eval_jaxpr/ppermute | solution.py:13
  18.9 9.3 %collective-permute-start.1 = (bf16[256,256]{1,0:T(8,128)(2,1)S(1)}, bf16[256,256]{1,0:T(8,128)(2,1)S(1)}, u32[]{:S(2)}, u32[]{:S(2)}) collective-permute-start(bf16[256,256]{1,0:T(8,128)(2,1)S(1)} %get-tuple-element.710), channel_id=1, source_target_pairs={{28,0},{0,4},{4,8},{8,12},{12,16},{16,20},{20,24},{24,28},{29,1},{... | collective-permute-start | bytes 393224 | tf_op jit(solution)/shard_map/while/body/eval_jaxpr/ppermute | solution.py:13
  19.0 7.9 %collective-permute-start = (s32[256]{0:T(256)S(1)}, s32[256]{0:T(256)S(1)}, u32[]{:S(2)}, u32[]{:S(2)}) collective-permute-start(s32[256]{0:T(256)S(1)} %get-tuple-element.711), channel_id=1, source_target_pairs={{28,0},{0,4},{4,8},{8,12},{12,16},{16,20},{20,24},{24,28},{29,1},{... | collective-permute-start | bytes 3080 | tf_op jit(solution)/shard_map/while/body/eval_jaxpr/ppermute | solution.py:13
  20.5 8.8 %collective-permute-start.3 = (bf16[256,256]{1,0:T(8,128)(2,1)S(1)}, bf16[256,256]{1,0:T(8,128)(2,1)S(1)}, u32[]{:S(2)}, u32[]{:S(2)}) collective-permute-start(bf16[256,256]{1,0:T(8,128)(2,1)S(1)} %get-tuple-element.712), channel_id=1, source_target_pairs={{4,0},{8,4},{12,8},{16,12},{20,16},{24,20},{28,24},{0,28},{5,1},{9... | collective-permute-start | bytes 393224 | tf_op jit(solution)/shard_map/while/body/eval_jaxpr/ppermute | solution.py:13
  23.8 4.5 %collective-permute-start.2 = (s32[256]{0:T(256)S(1)}, s32[256]{0:T(256)S(1)}, u32[]{:S(2)}, u32[]{:S(2)}) collective-permute-start(s32[256]{0:T(256)S(1)} %get-tuple-element.713), channel_id=1, source_target_pairs={{4,0},{8,4},{12,8},{16,12},{20,16},{24,20},{28,24},{0,28},{5,1},{9... | collective-permute-start | bytes 3080 | tf_op jit(solution)/shard_map/while/body/eval_jaxpr/ppermute | solution.py:13
  30.3 8.4 %collective-permute-start.1 = (bf16[256,256]{1,0:T(8,128)(2,1)S(1)}, bf16[256,256]{1,0:T(8,128)(2,1)S(1)}, u32[]{:S(2)}, u32[]{:S(2)}) collective-permute-start(bf16[256,256]{1,0:T(8,128)(2,1)S(1)} %get-tuple-element.710), channel_id=1, source_target_pairs={{28,0},{0,4},{4,8},{8,12},{12,16},{16,20},{20,24},{24,28},{29,1},{... | collective-permute-start | bytes 393224 | tf_op jit(solution)/shard_map/while/body/eval_jaxpr/ppermute | solution.py:13
  30.4 7.8 %collective-permute-start = (s32[256]{0:T(256)S(1)}, s32[256]{0:T(256)S(1)}, u32[]{:S(2)}, u32[]{:S(2)}) collective-permute-start(s32[256]{0:T(256)S(1)} %get-tuple-element.711), channel_id=1, source_target_pairs={{28,0},{0,4},{4,8},{8,12},{12,16},{16,20},{20,24},{24,28},{29,1},{... | collective-permute-start | bytes 3080 | tf_op jit(solution)/shard_map/while/body/eval_jaxpr/ppermute | solution.py:13
  31.4 8.3 %collective-permute-start.3 = (bf16[256,256]{1,0:T(8,128)(2,1)S(1)}, bf16[256,256]{1,0:T(8,128)(2,1)S(1)}, u32[]{:S(2)}, u32[]{:S(2)}) collective-permute-start(bf16[256,256]{1,0:T(8,128)(2,1)S(1)} %get-tuple-element.712), channel_id=1, source_target_pairs={{4,0},{8,4},{12,8},{16,12},{20,16},{24,20},{28,24},{0,28},{5,1},{9... | collective-permute-start | bytes 393224 | tf_op jit(solution)/shard_map/while/body/eval_jaxpr/ppermute | solution.py:13
  35.2 3.6 %collective-permute-start.2 = (s32[256]{0:T(256)S(1)}, s32[256]{0:T(256)S(1)}, u32[]{:S(2)}, u32[]{:S(2)}) collective-permute-start(s32[256]{0:T(256)S(1)} %get-tuple-element.713), channel_id=1, source_target_pairs={{4,0},{8,4},{12,8},{16,12},{20,16},{24,20},{28,24},{0,28},{5,1},{9... | collective-permute-start | bytes 3080 | tf_op jit(solution)/shard_map/while/body/eval_jaxpr/ppermute | solution.py:13
  40.9 8.5 %collective-permute-start.1 = (bf16[256,256]{1,0:T(8,128)(2,1)S(1)}, bf16[256,256]{1,0:T(8,128)(2,1)S(1)}, u32[]{:S(2)}, u32[]{:S(2)}) collective-permute-start(bf16[256,256]{1,0:T(8,128)(2,1)S(1)} %get-tuple-element.710), channel_id=1, source_target_pairs={{28,0},{0,4},{4,8},{8,12},{12,16},{16,20},{20,24},{24,28},{29,1},{... | collective-permute-start | bytes 393224 | tf_op jit(solution)/shard_map/while/body/eval_jaxpr/ppermute | solution.py:13
  41.1 7.7 %collective-permute-start = (s32[256]{0:T(256)S(1)}, s32[256]{0:T(256)S(1)}, u32[]{:S(2)}, u32[]{:S(2)}) collective-permute-start(s32[256]{0:T(256)S(1)} %get-tuple-element.711), channel_id=1, source_target_pairs={{28,0},{0,4},{4,8},{8,12},{12,16},{16,20},{20,24},{24,28},{29,1},{... | collective-permute-start | bytes 3080 | tf_op jit(solution)/shard_map/while/body/eval_jaxpr/ppermute | solution.py:13
  42.3 8.0 %collective-permute-start.3 = (bf16[256,256]{1,0:T(8,128)(2,1)S(1)}, bf16[256,256]{1,0:T(8,128)(2,1)S(1)}, u32[]{:S(2)}, u32[]{:S(2)}) collective-permute-start(bf16[256,256]{1,0:T(8,128)(2,1)S(1)} %get-tuple-element.712), channel_id=1, source_target_pairs={{4,0},{8,4},{12,8},{16,12},{20,16},{24,20},{28,24},{0,28},{5,1},{9... | collective-permute-start | bytes 393224 | tf_op jit(solution)/shard_map/while/body/eval_jaxpr/ppermute | solution.py:13
  45.8 3.6 %collective-permute-start.2 = (s32[256]{0:T(256)S(1)}, s32[256]{0:T(256)S(1)}, u32[]{:S(2)}, u32[]{:S(2)}) collective-permute-start(s32[256]{0:T(256)S(1)} %get-tuple-element.713), channel_id=1, source_target_pairs={{4,0},{8,4},{12,8},{16,12},{20,16},{24,20},{28,24},{0,28},{5,1},{9... | collective-permute-start | bytes 3080 | tf_op jit(solution)/shard_map/while/body/eval_jaxpr/ppermute | solution.py:13
  55.6 10.5 %copy-start.2 = (f32[4096]{0:T(1024)}, f32[4096]{0:T(1024)S(1)}, u32[]{:S(2)}) copy-start(f32[4096]{0:T(1024)S(1)} %all-gather) | copy-start | bytes 49156
  60.8 5.2 %copy-start.3 = (f32[4096]{0:T(1024)}, f32[4096]{0:T(1024)S(1)}, u32[]{:S(2)}) copy-start(f32[4096]{0:T(1024)S(1)} %all-gather.1) | copy-start | bytes 49156
  66.1 0.7 %slice-start = ((f32[4096]{0:T(1024)}), f32[1024]{0:T(1024)S(1)}, s32[]{:S(2)}) async-start(f32[4096]{0:T(1024)} %copy-done.2), calls=%async_computation | async-start | bytes 8192 | tf_op jit(solution)/shard_map/slice | solution.py:18
  66.1 0.7 slice-start.1
where the time goes:
time: 68 us; the launch traced here: 67.6 us
  starting transfers between devices  28.4 us (42%)
  blocking collectives  15.6 us (23%)
  waiting for transfers between devices  9.79 us (14%)
  other arithmetic  5.26 us (8%)
  matrix products  4.07 us (6%)
  local copies, waits for them, and re-layouts  3.63 us (5%)
  loops' own time  0.73 us (1%)
    ppermute x16, starting transfers between devices, passed_along(): return lax.ppermute(block, axis, route)  28.4 us
    all_gather x3, blocking collectives, merged(): pieces = jax.tree.map(lambda part: lax.all_gather(part, axis), value)  15.6 us
    ppermute x16, waiting for transfers between devices, passed_along(): return lax.ppermute(block, axis, route)  9.79 us
    reduce_sum x8, other arithmetic, score_block(): pos_logit = pos_logit + jnp.sum(jnp.where(is_pos, logits, 0.0), axis=1)  4.35 us
    dot_general x8, matrix products, score_block(): lax.dot_general(sources, block, (((1,), (1,)), ((), ())), preferred_eleme...  4.07 us
    unnamed x14, local copies, waits for them, and re-layouts  2.73 us
  transfers between devices with their start and end apart: 16, of which 8 were waited for; matrix products, arithmetic and copies ran while one was open for 6% of the time, Pallas kernels for 0%

commit v1 on v0

v1 whole, which is shorter than its diff:
```python
import functools

import jax
import jax.numpy as jnp
from jax import lax
from jax.experimental import pallas as pl
from jax.experimental.pallas import tpu as pltpu
from jax.sharding import PartitionSpec as P


SCALE = 3.0
NEG = -1e30
RATE = SCALE * 1.4426950408889634
LANES = 128
SUB = 8
CHUNK = 2 * LANES
AXES = ("blk", "grp")
VM = pl.BlockSpec(memory_space=pltpu.VMEM)
HB = pl.BlockSpec(memory_space=pltpu.HBM)


def tree(join, values):
    values = list(values)
    while len(values) > 1:
        values = [functools.reduce(join, values[k : k + 2]) for k in range(0, len(values), 2)]
    return values[0]


def call(body, out_shape, operands, scratch=(), flops=0, exps=0, space=VM):
    moved = sum(v.size * v.dtype.itemsize for v in [*operands, *jax.tree.leaves(out_shape)])
    return pl.pallas_call(
        body,
        out_shape=out_shape,
        in_specs=[space] * len(operands),
        out_specs=jax.tree.map(lambda _: VM, out_shape),
        scratch_shapes=list(scratch),
        compiler_params=pltpu.CompilerParams(vmem_limit_bytes=16 << 20),
        cost_estimate=pl.CostEstimate(flops=flops, transcendentals=exps, bytes_accessed=moved),
    )(*operands)


def prepare_body(destinations, dst_part, positive, src_part, packed, ids, parts, sems):
    rows = destinations.shape[0]
    half = positive.shape[0]
    moves = [
        (dst_part, parts),
        (destinations, packed.at[0:rows, :]),
        (positive, ids.at[0:half, :]),
        (src_part, ids.at[half : 2 * half, :]),
    ]
    copies = [pltpu.make_async_copy(*move, sems.at[k]) for k, move in enumerate(moves)]
    for copy in copies:
        copy.start()
    copies[0].wait()
    line = jnp.concatenate([parts[r : r + 1, :] for r in range(parts.shape[0])], axis=1)
    packed[rows : rows + SUB, :] = jnp.broadcast_to(line.astype(jnp.float32), (SUB, line.shape[1])).astype(packed.dtype)
    for copy in copies[1:]:
        copy.wait()


def set_column(piece, column, rows):
    line = piece[rows : rows + SUB, :].astype(jnp.float32)[0:1, :]
    for t in range(0, rows, LANES):
        column[t : t + LANES, :] = jnp.broadcast_to(line[:, t : t + LANES], (LANES, LANES)).T


def lane_group(logits, lane, column, row_ids, pos, part, carry):
    top, total, found = carry
    kept = []
    for t in range(0, logits.shape[0], SUB):
        x = logits[t : t + SUB, lane : lane + LANES]
        is_pos = row_ids[t : t + SUB, :] == pos
        found = jnp.where(is_pos, x, found)
        kept.append(jnp.where(is_pos, x, jnp.where(column[t : t + SUB, :] == part, NEG, x)))
    new = jnp.maximum(top, tree(jnp.maximum, kept))
    total = total * jnp.exp2((top - new) * RATE) + tree(jnp.add, [jnp.exp2((x - new) * RATE) for x in kept])
    return new, total, found


def fold_block(pieces, bases, columns, row_ids, block, before, finish):
    sources, ids = block
    count = sources.shape[0]
    rows = row_ids.shape[0]
    for i in range(0, count, CHUNK):
        logits = [
            lax.dot_general(
                piece[0:rows, :],
                sources[i : i + CHUNK, :],
                (((1,), (1,)), ((), ())),
                preferred_element_type=jnp.float32,
            )
            for piece in pieces
        ]
        for lane in range(0, CHUNK, LANES):
            g = (i + lane) // LANES
            h = count // LANES + g
            here = slice(i + lane, i + lane + LANES)
            part = jnp.broadcast_to(ids[h : h + 1, :], (SUB, LANES)).astype(jnp.float32)
            if before is None:
                carry = (jnp.full((SUB, LANES), NEG, jnp.float32),) + (jnp.zeros((SUB, LANES), jnp.float32),) * 2
            else:
                carry = tuple(before[SUB * r : SUB * (r + 1), here] for r in range(3))
            for p, base in enumerate(bases):
                pos = jnp.broadcast_to(ids[g : g + 1, :] - base, (SUB, LANES))
                carry = lane_group(logits[p], lane, columns.at[p], row_ids, pos, part, carry)
            finish(here, *carry)


def place():
    here = lax.axis_index("blk")
    return here // 2, here % 2, lax.axis_index("grp")


def base_of(z, rows):
    _, side, group = place()
    return ((z * 2 + side) * lax.axis_size("grp") + group) * rows


def pick(block, chosen=None):
    if len(block) == 2:
        return block
    group = place()[2]
    chosen[...] = jnp.where(group % 2 == 1, block[0][...], block[1][...])
    return chosen, block[2]


def gather_body(origins, n_block, resumed, *refs):
    n = len(origins)
    pieces, block = refs[:n], refs[n : n + n_block]
    before = refs[n + n_block] if resumed else None
    out, columns, row_ids, *chosen = refs[n + n_block + resumed :]
    rows = row_ids.shape[0]
    row_ids[...] = lax.broadcasted_iota(jnp.int32, row_ids.shape, 0)
    for p in range(n):
        set_column(pieces[p], columns.at[p], rows)

    def finish(here, *carry):
        for r, value in enumerate(carry):
            out[SUB * r : SUB * (r + 1), here] = value

    bases = [base_of(origin(place()[0]), rows) for origin in origins]
    fold_block(pieces, bases, columns, row_ids, pick(block, *chosen), before, finish)


def last_body(origin, outer, inner, own, own_ids, far, far_south, far_ids, own_before, far_before, out, *scratch):
    columns, row_ids, chosen, piece = scratch
    rows = row_ids.shape[0]
    spot = place()[0]
    ends = (spot == 0) | (spot == lax.axis_size("blk") // 2 - 1)
    piece[...] = jnp.where(ends, outer[...], inner[...])
    row_ids[...] = lax.broadcasted_iota(jnp.int32, row_ids.shape, 0)
    set_column(piece, columns.at[0], rows)
    blocks = (((own, own_ids), own_before), (pick((far, far_south, far_ids), chosen), far_before))
    for k, (block, before) in enumerate(blocks):

        def finish(here, top, total, found, k=k):
            peak = jnp.max(top, axis=0, keepdims=True)
            out[3 * k : 3 * k + 1, here] = peak
            out[3 * k + 1 : 3 * k + 2, here] = jnp.sum(
                total * jnp.exp2((top - peak) * RATE), axis=0, keepdims=True
            )
            out[3 * k + 2 : 3 * k + 3, here] = jnp.sum(found, axis=0, keepdims=True)

        fold_block([piece], [base_of(origin(spot), rows)], columns, row_ids, block, before, finish)


def joined(parts):
    peak = tree(jnp.maximum, [p[0] for p in parts])
    total = tree(jnp.add, [p[1] * jnp.exp2((p[0] - peak) * RATE) for p in parts])
    return peak, total, tree(jnp.add, [p[2] for p in parts])


def pair_body(mine, other, own_out, far_out):
    for k, out in ((0, own_out), (1, far_out)):
        parts = [tuple(v[3 * k + r : 3 * k + r + 1, :] for r in range(3)) for v in (mine, other)]
        for r, value in enumerate(joined(parts)):
            out[r : r + 1, :] = value


def final_body(*refs):
    out = refs[-1]
    peak, total, found = joined([tuple(ref[r : r + 1, :] for r in range(3)) for ref in refs[:-1]])
    loss = (peak - found) * SCALE + jnp.log(total)
    for i in range(out.shape[0]):
        out[i : i + 1, :] = loss[:, i * LANES : (i + 1) * LANES]


NEAR = {0: 2, 3: 1, 1: 0, 2: 3}
CROSS = {0: 1, 3: 2, 1: 3, 2: 0}
RELAY = {1: 0, 2: 3}


def source_of(route):
    return lambda z: sum(jnp.where(z == t, s, 0) for s, t in route.items())


def device_body(sources, positive, src_part, destinations, dst_part):
    rows, width = destinations.shape
    count = sources.shape[0]
    groups = lax.axis_size("grp")
    cycle = lax.axis_size("blk")
    line = cycle // 2

    def sent(value, move, take=lambda b, g: True):
        route = []
        for b in range(cycle):
            for g in range(groups):
                target = move(b // 2, b % 2, g) if take(b, g) else None
                if target is not None:
                    z, x, h = target
                    route.append((b * groups + g, (z * 2 + x) * groups + h))
        return lax.ppermute(value, AXES, route)

    def tiles(v):
        return v.reshape(-1, LANES)

    def shape(*dims):
        return jax.ShapeDtypeStruct(dims, jnp.float32)

    packed, ids = call(
        prepare_body,
        [
            jax.ShapeDtypeStruct((rows + SUB, width), destinations.dtype),
            jax.ShapeDtypeStruct((2 * count // LANES, LANES), jnp.int32),
        ],
        [destinations, tiles(dst_part), tiles(positive), tiles(src_part)],
        scratch=[pltpu.VMEM((rows // LANES, LANES), jnp.int32), pltpu.SemaphoreType.DMA((4,))],
        space=HB,
    )
    far = sent(sources, lambda z, x, g: (z, 1 - x, g), lambda b, g: g % 2 == 1)
    far_ids = sent(ids, lambda z, x, g: (z, 1 - x, g))
    far_south = sent(far, lambda z, x, g: (z, x, g - 1), lambda b, g: g % 2 == 1)
    block_copy = pltpu.VMEM(sources.shape, sources.dtype)

    def scratch(n):
        return [pltpu.VMEM((n, rows, LANES), jnp.float32), pltpu.VMEM((rows, LANES), jnp.int32)]

    def cost(n):
        return dict(flops=2 * n * rows * count * width, exps=n * rows * count)

    def gather(origins, pieces, block, before=None):
        return call(
            functools.partial(gather_body, origins, len(block), int(before is not None)),
            shape(3 * SUB, count),
            [*pieces, *block] + ([] if before is None else [before]),
            scratch(len(pieces)) + [block_copy] * (len(block) == 3),
            **cost(len(pieces)),
        )

    own_block = (sources, ids)
    far_block = (far, far_south, far_ids)
    mine = lambda z: z
    if line == 4:
        first = sent(packed, lambda z, x, g: (NEAR[z], x, g))
        second = sent(packed, lambda z, x, g: (CROSS[z], x, g))
        inner = sent(packed, lambda z, x, g: (3 - z, x, g) if z in RELAY else None)
        outer = sent(first, lambda z, x, g: (RELAY[z], x, g) if z in RELAY else None)
        from_first, from_second, origin = source_of(NEAR), source_of(CROSS), lambda z: line - 1 - z
        own_state = gather([mine], [packed], own_block)
        own_state = gather([from_first, from_second], [first, second], own_block, own_state)
        far_state = gather([mine, from_first, from_second], [packed, first, second], far_block)
    else:
        def turn(step, state):
            piece, own_state, far_state = state
            piece = sent(piece, lambda z, x, g: ((z + 1) % line, x, g))
            origin = [lambda z: (z - step) % line]
            own_state = gather(origin, [piece], own_block, own_state)
            far_state = gather(origin, [piece], far_block, far_state)
            return piece, own_state, far_state

        states = (gather([mine], [packed], own_block), gather([mine], [packed], far_block))
        state = (packed, *states)
        for step in range(1, line - 1):
            state = turn(step, state)
        outer, own_state, far_state = state
        outer = inner = sent(outer, lambda z, x, g: ((z + 1) % line, x, g))
        origin = lambda z: (z + 1) % line
    partial = call(
        functools.partial(last_body, origin),
        shape(8, count),
        [outer, inner, sources, ids, far, far_south, far_ids, own_state, far_state],
        scratch(1) + [block_copy, pltpu.VMEM(packed.shape, packed.dtype)],
        **cost(2),
    )
    partner = sent(partial, lambda z, x, g: (z, x, g ^ 1))
    near_sum, far_sum = call(pair_body, [shape(3, count)] * 2, [partial, partner])
    gathered = [near_sum]
    for hop in range(0, groups, 2):
        for flip in (1, 0):
            if hop or flip:
                value = far_sum if flip else near_sum
                gathered.append(sent(value, lambda z, x, g: (z, x ^ flip, g ^ hop)))
    loss = call(final_body, shape(count // LANES, LANES), gathered)
    return loss.reshape(count)


def solution(mesh):
    return jax.shard_map(
        device_body,
        mesh=mesh,
        in_specs=(P("blk", None), P("blk"), P("blk"), P(("blk", "grp"), None), P(("blk", "grp"))),
        out_specs=P("blk"),
        check_vma=False,
    )
```

time: 68 us -> 37.2 us (0.55)
  blocking collectives: 15.6 us -> 0 us
  starting transfers between devices: 28.4 us -> 21.8 us
  other arithmetic: 5.26 us -> 0 us
  Pallas kernels: 0 us -> 5.12 us
  matrix products: 4.07 us -> 0 us
  waiting for transfers between devices: 9.79 us -> 5.98 us
  loops' own time: 0.73 us -> 0 us
    all_gather x3 -> x0, blocking collectives: 15.6 us -> none  [merged(): pieces = jax.tree.map(lambda part: lax.all_gather(part, axis), value)]
    ppermute x16 -> x11, starting transfers between devices: 28.4 us -> 21.8 us  [sent(): return lax.ppermute(value, AXES, route)]
    pallas_call x0 -> x7, Pallas kernels: none -> 5.12 us  [call(): pl.pallas_call(body, out_shape=out_shape, in_specs=[space] * len(operands...]
    reduce_sum x8 -> x0, other arithmetic: 4.35 us -> none  [score_block(): pos_logit = pos_logit + jnp.sum(jnp.where(is_pos, logits, 0.0), axis=1)]
    dot_general x8 -> x0, matrix products: 4.07 us -> none  [score_block(): lax.dot_general(sources, block, (((1,), (1,)), ((), ())), preferred_eleme...]
    ppermute x16 -> x11, waiting for transfers between devices: 9.79 us -> 5.98 us  [sent(): return lax.ppermute(value, AXES, route)]
    unnamed x14 -> x12, local copies, waits for them, and re-layouts: 2.73 us -> 3.74 us
    another operation x6 -> x0, loops' own time: 0.73 us -> none  [the longest x1 0.37 us: on_device(): lax.fori_loop(1, half + 1, turn_both, (carry, destinations, dst_part, des...]
  transfers between devices with their start and end apart: 16 -> 11, of which waited for: 8 -> 5; matrix products, arithmetic and copies ran while one was open for 6% -> 0% of each run, Pallas kernels for 0% -> 9%
where the time goes in v1:
time: 37.2 us; the launch traced here: 36.8 us
  starting transfers between devices  21.8 us (59%)
  waiting for transfers between devices  5.98 us (16%)
  Pallas kernels  5.12 us (14%)
  local copies, waits for them, and re-layouts  3.74 us (10%)
    ppermute x11, starting transfers between devices, sent(): return lax.ppermute(value, AXES, route)  21.8 us
    ppermute x11, waiting for transfers between devices, sent(): return lax.ppermute(value, AXES, route)  5.98 us
    pallas_call x7, Pallas kernels, call(): pl.pallas_call(body, out_shape=out_shape, in_specs=[space] * len(operands...  5.12 us
    unnamed x12, local copies, waits for them, and re-layouts  3.74 us
  transfers between devices with their start and end apart: 11, of which 5 were waited for; matrix products, arithmetic and copies ran while one was open for 0% of the time, Pallas kernels for 9%

profile of v1, /device:TPU:0, one launch (start us, length us, event | category | flops | bytes accessed | tf_op | source)
XLA Modules:
  0.0 36.8 jit_solution(3153585825837401826)
XLA Ops:
  0.0 0.8 %collective-permute-start.3 = (bf16[1024,256]{1,0:T(8,128)(2,1)}, bf16[1024,256]{1,0:T(8,128)(2,1)S(1)}, u32[]{:S(2)}, u32[]{:S(2)}) collective-permute-start(bf16[1024,256]{1,0:T(8,128)(2,1)} %own.1), channel_id=1, source_target_pairs={{1,5},{3,7},{5,1},{7,3},{9,13},{11,15},{13,9},{15,11},{17,21},{19,... | collective-permute-start | bytes 1572872 | tf_op jit(solution)/shard_map/ppermute | solution.py:212
  0.8 1.3 %collective-permute-start.4 = (bf16[1024,256]{1,0:T(8,128)(2,1)S(1)}, bf16[1024,256]{1,0:T(8,128)(2,1)S(1)}, u32[]{:S(2)}, u32[]{:S(2)}) collective-permute-start(bf16[1024,256]{1,0:T(8,128)(2,1)S(1)} %collective-permute-done.3.refs_3_.far), channel_id=1, source_target_pairs={{1,0},{3,2},{5,4},{7,6},{9,8},{11,10},{13,12},{15,14},{17,16},{19,... | collective-permute-start | bytes 1572872 | tf_op jit(solution)/shard_map/ppermute | solution.py:212
  2.2 0.7 %copy-done.5 = s32[256]{0:T(256)S(1)} copy-done((s32[256]{0:T(256)S(1)}, s32[256]{0:T(256)}, u32[]{:S(2)}) %copy-start.5) | copy-done | bytes 1048
  2.8 0.9 %copy-done.2 = bf16[256,256]{1,0:T(8,128)(2,1)S(1)} copy-done((bf16[256,256]{1,0:T(8,128)(2,1)S(1)}, bf16[256,256]{1,0:T(8,128)(2,1)}, u32[]{:S(2)}) %copy-start.2) | copy-done | bytes 131096
  3.7 0.7 %copy-done.4 = s32[1024]{0:T(1024)S(1)} copy-done((s32[1024]{0:T(1024)S(1)}, s32[1024]{0:T(1024)}, u32[]{:S(2)}) %copy-start.4) | copy-done | bytes 4120
  4.6 4.1 %collective-permute-start = (bf16[264,256]{1,0:T(8,128)(2,1)S(1)}, bf16[264,256]{1,0:T(8,128)(2,1)S(1)}, u32[]{:S(2)}, u32[]{:S(2)}) collective-permute-start(bf16[264,256]{1,0:T(8,128)(2,1)S(1)} %get-tuple-element.9.refs_0_), channel_id=1, source_target_pairs={{0,16},{1,17},{2,18},{3,19},{4,20},{5,21},{6,22},{7,23},{8,0},{9,1... | collective-permute-start | bytes 405512 | tf_op jit(solution)/shard_map/ppermute | solution.py:212
  8.7 0.7 %collective-permute-start.2 = (bf16[264,256]{1,0:T(8,128)(2,1)S(1)}, bf16[264,256]{1,0:T(8,128)(2,1)S(1)}, u32[]{:S(2)}, u32[]{:S(2)}) collective-permute-start(bf16[264,256]{1,0:T(8,128)(2,1)S(1)} %get-tuple-element.9.refs_0_), channel_id=1, source_target_pairs={{8,16},{9,17},{10,18},{11,19},{12,20},{13,21},{14,22},{15,23},{16,... | collective-permute-start | bytes 405512 | tf_op jit(solution)/shard_map/ppermute | solution.py:212
  9.4 1.9 %collective-permute-done.refs_0_.refs_1_ = bf16[264,256]{1,0:T(8,128)(2,1)S(1)} collective-permute-done((bf16[264,256]{1,0:T(8,128)(2,1)S(1)}, bf16[264,256]{1,0:T(8,128)(2,1)S(1)}, u32[]{:S(2)}, u32[]{:S(2)}) %collective-permute-start) | collective-permute-done | bytes 135200 | tf_op jit(solution)/shard_map/ppermute | solution.py:212
  11.3 1.3 %collective-permute-start.1 = (bf16[264,256]{1,0:T(8,128)(2,1)S(1)}, bf16[264,256]{1,0:T(8,128)(2,1)S(1)}, u32[]{:S(2)}, u32[]{:S(2)}) collective-permute-start(bf16[264,256]{1,0:T(8,128)(2,1)S(1)} %collective-permute-done.refs_0_.refs_1_), channel_id=1, source_target_pairs={{8,0},{9,1},{10,2},{11,3},{12,4},{13,5},{14,6},{15,7},{16,24},{17,... | collective-permute-start | bytes 405512 | tf_op jit(solution)/shard_map/ppermute | solution.py:212
  12.6 1.6 %collective-permute-start.5 = (s32[16,128]{1,0:T(8,128)S(1)}, s32[16,128]{1,0:T(8,128)S(1)}, u32[]{:S(2)}, u32[]{:S(2)}) collective-permute-start(s32[16,128]{1,0:T(8,128)S(1)} %get-tuple-element.10.refs_2_.refs_3_.own_ids), channel_id=1, source_target_pairs={{0,4},{1,5},{2,6},{3,7},{4,0},{5,1},{6,2},{7,3},{8,12},{9,13},{10,... | collective-permute-start | bytes 24584 | tf_op jit(solution)/shard_map/ppermute | solution.py:212
  14.1 1.0 %copy-done = bf16[1024,256]{1,0:T(8,128)(2,1)S(1)} copy-done((bf16[1024,256]{1,0:T(8,128)(2,1)S(1)}, bf16[1024,256]{1,0:T(8,128)(2,1)}, u32[]{:S(2)}) %copy-start) | copy-done | bytes 524312
  15.2 0.6 %shard_map.56.refs_4_ = f32[24,1024]{1,0:T(8,128)S(1)} custom-call(bf16[264,256]{1,0:T(8,128)(2,1)S(1)} %get-tuple-element.9.refs_0_, bf16[1024,256]{1,0:T(8,128)(2,1)S(1)} %copy-done, s32[16,128]{1,0:T(8,128)S(1)} %get-tuple-element.10.refs_2_.refs_3_.own_ids), custom_call_target="tpu_custom_call" | custom-call | flops 134217728 | bytes 765952 | tf_op jit(solution)/shard_map/pallas_call | solution.py:31
  15.8 0.4 %copy-done.1 = bf16[1024,256]{1,0:T(8,128)(2,1)S(1)} copy-done((bf16[1024,256]{1,0:T(8,128)(2,1)S(1)}, bf16[1024,256]{1,0:T(8,128)(2,1)}, u32[]{:S(2)}) %copy-start.1) | copy-done | bytes 524312
  16.2 1.1 %shard_map.57.own_before = f32[24,1024]{1,0:T(8,128)S(1)} custom-call(bf16[264,256]{1,0:T(8,128)(2,1)S(1)} %collective-permute-done.refs_0_.refs_1_, bf16[264,256]{1,0:T(8,128)(2,1)S(1)} %collective-permute-done.6.refs_1_.refs_2_, bf16[1024,256]{1,0:T(8,128)(2,1)S(1)} %copy-done.1, s32[16,128]{1,0:T(8,128)S(1)} %get-tuple-element.10.refs_2_.refs_3_.own_ids, ...), custom_call_target="tpu_custom_call" | custom-call | flops 268435456 | bytes 999424 | tf_op jit(solution)/shard_map/pallas_call | solution.py:31
  17.3 1.6 %shard_map.58.far_before = f32[24,1024]{1,0:T(8,128)S(1)} custom-call(bf16[264,256]{1,0:T(8,128)(2,1)S(1)} %get-tuple-element.9.refs_0_, bf16[264,256]{1,0:T(8,128)(2,1)S(1)} %collective-permute-done.refs_0_.refs_1_, bf16[264,256]{1,0:T(8,128)(2,1)S(1)} %collective-permute-done.6.refs_1_.refs_2_, bf16[1024,256]{1,0:T(8,128)(2,1)S(1)} %collective-permute-done.3.refs_3_.far, ...), custom_call_target="tpu_custom_call" | custom-call | flops 402653184 | bytes 1560576 | tf_op jit(solution)/shard_map/pallas_call | solution.py:31
  18.9 1.1 %shard_map.59.mine = f32[8,1024]{1,0:T(8,128)S(1)} custom-call(bf16[264,256]{1,0:T(8,128)(2,1)S(1)} %collective-permute-done.1.outer, bf16[264,256]{1,0:T(8,128)(2,1)S(1)} %collective-permute-done.2.inner, bf16[1024,256]{1,0:T(8,128)(2,1)S(1)} %copy-done.1, s32[16,128]{1,0:T(8,128)S(1)} %get-tuple-element.10.refs_2_.refs_3_.own_ids, ...), custom_call_target="tpu_custom_call" | custom-call | flops 268435456 | bytes 2088960 | tf_op jit(solution)/shard_map/pallas_call | solution.py:31
  20.0 8.5 %collective-permute-start.7 = (f32[8,1024]{1,0:T(8,128)S(1)}, f32[8,1024]{1,0:T(8,128)S(1)}, u32[]{:S(2)}, u32[]{:S(2)}) collective-permute-start(f32[8,1024]{1,0:T(8,128)S(1)} %shard_map.59.mine), channel_id=1, source_target_pairs={{0,1},{1,0},{2,3},{3,2},{4,5},{5,4},{6,7},{7,6},{8,9},{9,8},{10,11... | collective-permute-start | bytes 98312 | tf_op jit(solution)/shard_map/ppermute | solution.py:212
  28.5 0.9 %collective-permute-done.7.other = f32[8,1024]{1,0:T(8,128)S(1)} collective-permute-done((f32[8,1024]{1,0:T(8,128)S(1)}, f32[8,1024]{1,0:T(8,128)S(1)}, u32[]{:S(2)}, u32[]{:S(2)}) %collective-permute-start.7) | collective-permute-done | bytes 32800 | tf_op jit(solution)/shard_map/ppermute | solution.py:212
  29.4 1.6 %collective-permute-start.10 = (f32[3,1024]{1,0:T(4,128)S(1)}, f32[3,1024]{1,0:T(4,128)S(1)}, u32[]{:S(2)}, u32[]{:S(2)}) collective-permute-start(f32[3,1024]{1,0:T(4,128)S(1)} %get-tuple-element.11.refs_0_), channel_id=1, source_target_pairs={{0,2},{1,3},{2,0},{3,1},{4,6},{5,7},{6,4},{7,5},{8,10},{9,11},{10,... | collective-permute-start | bytes 36872 | tf_op jit(solution)/shard_map/ppermute | solution.py:212
  30.9 0.5 %collective-permute-start.8 = (f32[3,1024]{1,0:T(4,128)S(1)}, f32[3,1024]{1,0:T(4,128)S(1)}, u32[]{:S(2)}, u32[]{:S(2)}) collective-permute-start(f32[3,1024]{1,0:T(4,128)S(1)} %get-tuple-element.12), channel_id=1, source_target_pairs={{0,4},{1,5},{2,6},{3,7},{4,0},{5,1},{6,2},{7,3},{8,12},{9,13},{10,... | collective-permute-start | bytes 36872 | tf_op jit(solution)/shard_map/ppermute | solution.py:212
  31.5 1.4 %collective-permute-start.9 = (f32[3,1024]{1,0:T(4,128)S(1)}, f32[3,1024]{1,0:T(4,128)S(1)}, u32[]{:S(2)}, u32[]{:S(2)}) collective-permute-start(f32[3,1024]{1,0:T(4,128)S(1)} %get-tuple-element.12), channel_id=1, source_target_pairs={{0,6},{1,7},{2,4},{3,5},{4,2},{5,3},{6,0},{7,1},{8,14},{9,15},{10,... | collective-permute-start | bytes 36872 | tf_op jit(solution)/shard_map/ppermute | solution.py:212
  33.2 1.5 %collective-permute-done.8.refs_1_ = f32[3,1024]{1,0:T(4,128)S(1)} collective-permute-done((f32[3,1024]{1,0:T(4,128)S(1)}, f32[3,1024]{1,0:T(4,128)S(1)}, u32[]{:S(2)}, u32[]{:S(2)}) %collective-permute-start.8) | collective-permute-done | bytes 12320 | tf_op jit(solution)/shard_map/ppermute | solution.py:212
  34.7 1.4 %collective-permute-done.9.refs_2_ = f32[3,1024]{1,0:T(4,128)S(1)} collective-permute-done((f32[3,1024]{1,0:T(4,128)S(1)}, f32[3,1024]{1,0:T(4,128)S(1)}, u32[]{:S(2)}, u32[]{:S(2)}) %collective-permute-start.9) | collective-permute-done | bytes 12320 | tf_op jit(solution)/shard_map/ppermute | solution.py:212
  36.1 0.6 %shard_map.61 = f32[8,128]{1,0:T(8,128)} custom-call(f32[3,1024]{1,0:T(4,128)S(1)} %get-tuple-element.11.refs_0_, f32[3,1024]{1,0:T(4,128)S(1)} %collective-permute-done.8.refs_1_, f32[3,1024]{1,0:T(4,128)S(1)} %collective-permute-done.9.refs_2_, f32[3,1024]{1,0:T(4,128)S(1)} %collective-permute-done.10.refs_3_), custom_call_target="tpu_custom_call" | custom-call | bytes 53248 | tf_op jit(solution)/shard_map/pallas_call | solution.py:31
  (17 shorter events, 0.5 us)
Async XLA Ops:
  0.0 2.1 %copy-start.3 = (s32[1024]{0:T(1024)S(1)}, s32[1024]{0:T(1024)}, u32[]{:S(2)}) copy-start(s32[1024]{0:T(1024)} %param.6) | copy-start | bytes 12292
  0.0 0.8 %collective-permute-start.3 = (bf16[1024,256]{1,0:T(8,128)(2,1)}, bf16[1024,256]{1,0:T(8,128)(2,1)S(1)}, u32[]{:S(2)}, u32[]{:S(2)}) collective-permute-start(bf16[1024,256]{1,0:T(8,128)(2,1)} %own.1), channel_id=1, source_target_pairs={{1,5},{3,7},{5,1},{7,3},{9,13},{11,15},{13,9},{15,11},{17,21},{19,... | collective-permute-start | bytes 1572872 | tf_op jit(solution)/shard_map/ppermute | solution.py:212
  0.8 16.5 %collective-permute-start.4 = (bf16[1024,256]{1,0:T(8,128)(2,1)S(1)}, bf16[1024,256]{1,0:T(8,128)(2,1)S(1)}, u32[]{:S(2)}, u32[]{:S(2)}) collective-permute-start(bf16[1024,256]{1,0:T(8,128)(2,1)S(1)} %collective-permute-done.3.refs_3_.far), channel_id=1, source_target_pairs={{1,0},{3,2},{5,4},{7,6},{9,8},{11,10},{13,12},{15,14},{17,16},{19,... | collective-permute-start | bytes 1572872 | tf_op jit(solution)/shard_map/ppermute | solution.py:212
  2.1 0.7 %copy-start.5 = (s32[256]{0:T(256)S(1)}, s32[256]{0:T(256)}, u32[]{:S(2)}) copy-start(s32[256]{0:T(256)} %param.9) | copy-start | bytes 3076
  2.8 0.9 %copy-start.2 = (bf16[256,256]{1,0:T(8,128)(2,1)S(1)}, bf16[256,256]{1,0:T(8,128)(2,1)}, u32[]{:S(2)}) copy-start(bf16[256,256]{1,0:T(8,128)(2,1)} %destinations.1) | copy-start | bytes 393220
  3.7 0.7 %copy-start.4 = (s32[1024]{0:T(1024)S(1)}, s32[1024]{0:T(1024)}, u32[]{:S(2)}) copy-start(s32[1024]{0:T(1024)} %param.7) | copy-start | bytes 12292
  4.6 6.7 %collective-permute-start = (bf16[264,256]{1,0:T(8,128)(2,1)S(1)}, bf16[264,256]{1,0:T(8,128)(2,1)S(1)}, u32[]{:S(2)}, u32[]{:S(2)}) collective-permute-start(bf16[264,256]{1,0:T(8,128)(2,1)S(1)} %get-tuple-element.9.refs_0_), channel_id=1, source_target_pairs={{0,16},{1,17},{2,18},{3,19},{4,20},{5,21},{6,22},{7,23},{8,0},{9,1... | collective-permute-start | bytes 405512 | tf_op jit(solution)/shard_map/ppermute | solution.py:212
  8.7 7.0 %collective-permute-start.6 = (bf16[264,256]{1,0:T(8,128)(2,1)S(1)}, bf16[264,256]{1,0:T(8,128)(2,1)S(1)}, u32[]{:S(2)}, u32[]{:S(2)}) collective-permute-start(bf16[264,256]{1,0:T(8,128)(2,1)S(1)} %get-tuple-element.9.refs_0_), channel_id=1, source_target_pairs={{0,8},{1,9},{2,10},{3,11},{4,12},{5,13},{6,14},{7,15},{8,24},{9,25... | collective-permute-start | bytes 405512 | tf_op jit(solution)/shard_map/ppermute | solution.py:212
  8.7 10.2 %collective-permute-start.2 = (bf16[264,256]{1,0:T(8,128)(2,1)S(1)}, bf16[264,256]{1,0:T(8,128)(2,1)S(1)}, u32[]{:S(2)}, u32[]{:S(2)}) collective-permute-start(bf16[264,256]{1,0:T(8,128)(2,1)S(1)} %get-tuple-element.9.refs_0_), channel_id=1, source_target_pairs={{8,16},{9,17},{10,18},{11,19},{12,20},{13,21},{14,22},{15,23},{16,... | collective-permute-start | bytes 405512 | tf_op jit(solution)/shard_map/ppermute | solution.py:212
  11.3 7.6 %collective-permute-start.1 = (bf16[264,256]{1,0:T(8,128)(2,1)S(1)}, bf16[264,256]{1,0:T(8,128)(2,1)S(1)}, u32[]{:S(2)}, u32[]{:S(2)}) collective-permute-start(bf16[264,256]{1,0:T(8,128)(2,1)S(1)} %collective-permute-done.refs_0_.refs_1_), channel_id=1, source_target_pairs={{8,0},{9,1},{10,2},{11,3},{12,4},{13,5},{14,6},{15,7},{16,24},{17,... | collective-permute-start | bytes 405512 | tf_op jit(solution)/shard_map/ppermute | solution.py:212
  12.6 4.7 %collective-permute-start.5 = (s32[16,128]{1,0:T(8,128)S(1)}, s32[16,128]{1,0:T(8,128)S(1)}, u32[]{:S(2)}, u32[]{:S(2)}) collective-permute-start(s32[16,128]{1,0:T(8,128)S(1)} %get-tuple-element.10.refs_2_.refs_3_.own_ids), channel_id=1, source_target_pairs={{0,4},{1,5},{2,6},{3,7},{4,0},{5,1},{6,2},{7,3},{8,12},{9,13},{10,... | collective-permute-start | bytes 24584 | tf_op jit(solution)/shard_map/ppermute | solution.py:212
  14.1 1.0 %copy-start = (bf16[1024,256]{1,0:T(8,128)(2,1)S(1)}, bf16[1024,256]{1,0:T(8,128)(2,1)}, u32[]{:S(2)}) copy-start(bf16[1024,256]{1,0:T(8,128)(2,1)} %own.1) | copy-start | bytes 1572868
  15.2 1.0 %copy-start.1 = (bf16[1024,256]{1,0:T(8,128)(2,1)S(1)}, bf16[1024,256]{1,0:T(8,128)(2,1)}, u32[]{:S(2)}) copy-start(bf16[1024,256]{1,0:T(8,128)(2,1)} %own.1) | copy-start | bytes 1572868
  20.0 9.4 %collective-permute-start.7 = (f32[8,1024]{1,0:T(8,128)S(1)}, f32[8,1024]{1,0:T(8,128)S(1)}, u32[]{:S(2)}, u32[]{:S(2)}) collective-permute-start(f32[8,1024]{1,0:T(8,128)S(1)} %shard_map.59.mine), channel_id=1, source_target_pairs={{0,1},{1,0},{2,3},{3,2},{4,5},{5,4},{6,7},{7,6},{8,9},{9,8},{10,11... | collective-permute-start | bytes 98312 | tf_op jit(solution)/shard_map/ppermute | solution.py:212
  29.4 3.8 %collective-permute-start.10 = (f32[3,1024]{1,0:T(4,128)S(1)}, f32[3,1024]{1,0:T(4,128)S(1)}, u32[]{:S(2)}, u32[]{:S(2)}) collective-permute-start(f32[3,1024]{1,0:T(4,128)S(1)} %get-tuple-element.11.refs_0_), channel_id=1, source_target_pairs={{0,2},{1,3},{2,0},{3,1},{4,6},{5,7},{6,4},{7,5},{8,10},{9,11},{10,... | collective-permute-start | bytes 36872 | tf_op jit(solution)/shard_map/ppermute | solution.py:212
  30.9 3.7 %collective-permute-start.8 = (f32[3,1024]{1,0:T(4,128)S(1)}, f32[3,1024]{1,0:T(4,128)S(1)}, u32[]{:S(2)}, u32[]{:S(2)}) collective-permute-start(f32[3,1024]{1,0:T(4,128)S(1)} %get-tuple-element.12), channel_id=1, source_target_pairs={{0,4},{1,5},{2,6},{3,7},{4,0},{5,1},{6,2},{7,3},{8,12},{9,13},{10,... | collective-permute-start | bytes 36872 | tf_op jit(solution)/shard_map/ppermute | solution.py:212
  31.5 4.6 %collective-permute-start.9 = (f32[3,1024]{1,0:T(4,128)S(1)}, f32[3,1024]{1,0:T(4,128)S(1)}, u32[]{:S(2)}, u32[]{:S(2)}) collective-permute-start(f32[3,1024]{1,0:T(4,128)S(1)} %get-tuple-element.12), channel_id=1, source_target_pairs={{0,6},{1,7},{2,4},{3,5},{4,2},{5,3},{6,0},{7,1},{8,14},{9,15},{10,... | collective-permute-start | bytes 36872 | tf_op jit(solution)/shard_map/ppermute | solution.py:212
